TPU v7x, 32 devices: a whole 2x2x4 slice. The times are simulated.
32 devices in a mesh: shots: 2 (over y), rx: 4 (over z), ta: 2 (over x), af: 2 (over core).
Axes of the slice: x: 2, y: 2, z: 4, core: 2. Of those that a mesh axis runs over, the one named last changes fastest.
Arguments:
- traces: bfloat16 [4096, 512], P(('shots', 'rx'), ('ta', 'af')), parts along dimension 0, may hold values from -6 to 6
- slopes: int32 [512], replicated, may hold values from 0 to 1023
- offsets: int32 [4096], P('shots'), parts along dimension 0, may hold values from 1 to 4095
- live: int32 [4096], P('shots'), parts along dimension 0, may hold values 0 or 1
Outputs:
- stack: float32 [1024, 512], P(('shots', 'rx'), ('ta', 'af')), parts along dimension 0
- coherence: float32 [1024, 512], P(('shots', 'rx'), ('ta', 'af')), parts along dimension 0
- peak_values: float32 [1024], P(('shots', 'rx')), parts along dimension 0
There are 2 independent parts, one for each index of `shots`. A program takes and returns all parts, laid end to end along the dimension named above; an argument that names none is the same for every part. Nothing has to cross between parts.
Inputs may be any that keep to these rules, and one draw needn't show every extreme that they name: delays are below 64: (slopes * offsets) // 65536 < 64.
All inputs are finite; a program needn't handle non-finite values.
Results may differ from a plain program's by a relative error of at most 0.0003.
Values may be sent and summed in bfloat16 or wider, within the bound.
No kernel may reach another device: no remote copies, remote signals or barrier semaphores. Data moves between devices by JAX's collectives and lax.ppermute only.
A program may use at most 64 MiB of HBM per device.

v0:
```python
import jax
import jax.numpy as jnp
from jax import lax
from jax.sharding import PartitionSpec as P

SPAN = 64
WIN = 16


def passed_along(value, axis, steps):
    count = lax.axis_size(axis)
    leading, last = (max(0, -steps), min(count, count - steps))
    return lax.ppermute(value, axis, [(source, source + steps) for source in range(leading, last)])


def hankel(samples, delay_span, block_len):
    row_total, length = samples.shape
    repeated = jnp.tile(samples, (1, delay_span))
    repeated = jnp.pad(repeated, ((0, 0), (0, delay_span)))
    return repeated.reshape(row_total, delay_span, length + 1)[:, :, :block_len]


def build_lagged(samples, delay_span, block_len):
    squared = (samples.astype(jnp.float32) ** 2).astype(jnp.bfloat16)
    return (hankel(samples, delay_span, block_len), hankel(squared, delay_span, block_len))


def project_lags(slope_rows, offset_rows, lagged_x, lagged_s, delay_span):
    delays = slope_rows[:, None] * offset_rows[None, :] // 65536
    lags = jnp.arange(delay_span, dtype=jnp.int32)
    onehot = (delays[:, :, None] == lags[None, None, :]).astype(jnp.bfloat16)
    stacked = jnp.einsum("prk,rkt->pt", onehot, lagged_x, preferred_element_type=jnp.float32)
    energy = jnp.einsum("prk,rkt->pt", onehot, lagged_s, preferred_element_type=jnp.float32)
    return jnp.concatenate([stacked, energy], axis=1)


def on_device(traces, slopes, offsets, live):
    receiver_group = lax.axis_index("rx")
    local_rows, block_len = traces.shape
    delay_span = SPAN
    window = WIN
    live_gain = lax.dynamic_slice_in_dim(live, receiver_group * local_rows, local_rows).astype(
        jnp.bfloat16
    )
    offset_local = lax.dynamic_slice_in_dim(offsets, receiver_group * local_rows, local_rows)
    weighted = traces * live_gain[:, None]
    arriving = passed_along(weighted[:, :delay_span], ("ta", "af"), -1)
    extended = jnp.concatenate([weighted, arriving], axis=1)
    local_x, local_s = build_lagged(extended, delay_span, block_len)
    summed = lax.psum_scatter(
        project_lags(slopes, offset_local, local_x, local_s, delay_span),
        "rx",
        scatter_dimension=0,
        tiled=True,
    )
    stack = summed[:, :block_len]
    energy = summed[:, block_len:]
    following = passed_along((stack[:, :window], energy[:, :window]), ("ta", "af"), -1)
    long_stack = jnp.concatenate([stack, following[0]], axis=1)
    long_energy = jnp.concatenate([energy, following[1]], axis=1)
    power_sum = jnp.zeros_like(stack)
    energy_sum = jnp.zeros_like(energy)
    for lag_index in range(window):
        power_sum = power_sum + long_stack[:, lag_index : lag_index + block_len] ** 2
        energy_sum = energy_sum + long_energy[:, lag_index : lag_index + block_len]
    coherence = power_sum / jnp.maximum(energy_sum, 1.0)
    peak_values = lax.pmax(jnp.max(coherence, axis=1), ("ta", "af"))
    return (stack, coherence, peak_values)


def solution(mesh):
    placed = (P(("shots", "rx"), ("ta", "af")), P(), P("shots"), P("shots"))
    return jax.shard_map(
        on_device,
        mesh=mesh,
        in_specs=placed,
        out_specs=(
            P(("shots", "rx"), ("ta", "af")),
            P(("shots", "rx"), ("ta", "af")),
            P(("shots", "rx")),
        ),
        check_vma=False,
    )
```

profile of v0, /device:TPU:0, one launch (start us, length us, event | category | flops | bytes accessed | tf_op | source)
XLA Modules:
  0.0 147.2 jit_solution(1106759283798716717)
XLA Ops:
  7.2 0.0 reduce-scatter.2.cloned.1.call-start
  7.2 1.0 copy.15
  8.2 0.8 dynamic-slice_convert_fusion
  9.0 1.3 collective-permute-start
  10.3 0.8 dynamic_slice.6
  11.1 1.4 add_select_fusion
  12.5 0.0 collective-permute-done
  12.5 6.1 %tile.8 = bf16[512,64,192]{0,2,1:T(8,128)(2,1)} broadcast(bf16[512,192]{0,1:T(8,128)(2,1)S(1)} %pad_maximum_fusion.1), dimensions={0,2} | broadcast | bytes 12779520 | tf_op jit(solution)/shard_map/tile | solution.py:18
  18.6 10.6 %pad.7 = bf16[512,12352]{0,1:T(8,128)(2,1)} pad(bf16[512,12288]{0,1:T(8,128)(2,1)} %bitcast.11, bf16[]{:T(256)} %constant.29.clone.1), padding=0_0x0_64 | pad | bytes 25231362 | tf_op jit(solution)/shard_map/jit(_pad)/pad | solution.py:19
  29.1 12.8 %reshape.79 = bf16[512,64,193]{0,2,1:T(8,128)(2,1)} reshape(bf16[512,12352]{0,1:T(8,128)(2,1)} %pad.7) | data formatting | bytes 25296896 | tf_op jit(solution)/shard_map/reshape | solution.py:20
  41.9 6.0 %tile.20 = bf16[512,64,192]{0,2,1:T(8,128)(2,1)} broadcast(bf16[512,192]{0,1:T(8,128)(2,1)S(1)} %multiply_convert_fusion), dimensions={0,2} | broadcast | bytes 12779520 | tf_op jit(solution)/shard_map/tile | solution.py:18
  48.0 10.5 %pad.8 = bf16[512,12352]{0,1:T(8,128)(2,1)} pad(bf16[512,12288]{0,1:T(8,128)(2,1)} %bitcast.10, bf16[]{:T(256)} %constant.29.clone.1), padding=0_0x0_64 | pad | bytes 25231362 | tf_op jit(solution)/shard_map/jit(_pad)/pad | solution.py:19
  58.5 12.8 %reshape.80 = bf16[512,64,193]{0,2,1:T(8,128)(2,1)} reshape(bf16[512,12352]{0,1:T(8,128)(2,1)} %pad.8) | data formatting | bytes 25296896 | tf_op jit(solution)/shard_map/reshape | solution.py:20
  71.3 0.0 copy-start
  71.3 14.7 %fusion.6 = f32[512,128]{0,1:T(8,128)S(1)} fusion(bf16[512,64,193]{0,2,1:T(8,128)(2,1)} %reshape.79, s32[512,512]{1,0:T(8,128)S(1)} %add_select_fusion), kind=kOutput, calls=%fused_computation.14 | convolution fusion | flops 4311744512 | bytes 9699328 | tf_op jit(solution)/shard_map/prk,rkt->pt/dot_general | solution.py:32
  86.0 0.0 copy-done
  86.0 12.9 %fusion.9 = f32[512,128]{0,1:T(8,128)S(1)} fusion(bf16[512,64,193]{0,2,1:T(8,128)(2,1)S(1)} %copy-done, s32[512,512]{1,0:T(8,128)S(1)} %add_select_fusion), kind=kOutput, calls=%fused_computation.15 | convolution fusion | flops 4311744512 | bytes 9699328 | tf_op jit(solution)/shard_map/prk,rkt->pt/dot_general | solution.py:33
  98.8 0.8 pad_maximum_fusion
  99.7 0.0 reduce-scatter.2.cloned.1.call-update
  99.7 25.5 %reduce-scatter.2.cloned.1.call-done = f32[128,256]{0,1:T(8,128)} async-done(((f32[512,256]{0,1:T(8,128)}), f32[128,256]{0,1:T(8,128)}) %reduce-scatter.2.cloned.1.call-update) | async-done | bytes 131088 | tf_op jit(solution)/shard_map/reduce_scatter | solution.py:50
  125.2 0.7 fusion.94
  125.9 1.3 collective-permute-start.1
  127.2 1.3 collective-permute-start.2
  128.5 0.9 fusion.95
  129.4 0.7 copy.16
  130.1 0.0 collective-permute-done.1
  130.1 0.8 collective-permute-done.2
  130.9 0.2 fusion.92
  131.1 8.6 %pmax.7 = f32[128]{0:T(128)} all-reduce(f32[128]{0:T(128)S(1)} %get-tuple-element.12), channel_id=1, replica_groups=mesh['shots'=2,'rx'=4,'ta'=2,'af'=2] {'ta','af'}, use_global_device_ids=true, to_apply=%region_2.3 | all-reduce | flops 128 | bytes 1024 | tf_op jit(solution)/shard_map/pmax | solution.py:67
  139.6 0.7 copy.17
  (4 shorter events, 0.1 us)
Async XLA Ops:
  7.2 118.0 %reduce-scatter.2.cloned.1.call-start = ((), (), s32[]{:S(2)}) async-start(), calls=%async_computation.1 | async-start | bytes 655360 | tf_op jit(solution)/shard_map/reduce_scatter | solution.py:50
  9.0 3.4 %collective-permute-start = (bf16[512,64]{0,1:T(8,128)(2,1)S(1)}, bf16[512,64]{0,1:T(8,128)(2,1)S(1)}, u32[]{:S(2)}, u32[]{:S(2)}) collective-permute-start(bf16[512,64]{0,1:T(8,128)(2,1)S(1)} %slice.150), channel_id=1, source_target_pairs={{1,0},{2,1},{3,2},{5,4},{6,5},{7,6},{9,8},{10,9},{11,10},{13,12},{... | collective-permute-start | bytes 196616 | tf_op jit(solution)/shard_map/ppermute | solution.py:13
  71.3 14.7 %copy-start = (bf16[512,64,193]{0,2,1:T(8,128)(2,1)S(1)}, bf16[512,64,193]{0,2,1:T(8,128)(2,1)}, u32[]{:S(2)}) copy-start(bf16[512,64,193]{0,2,1:T(8,128)(2,1)} %reshape.80) | copy-start | bytes 37945348
  125.9 4.2 %collective-permute-start.1 = (f32[128,16]{0,1:T(8,128)S(1)}, f32[128,16]{0,1:T(8,128)S(1)}, u32[]{:S(2)}, u32[]{:S(2)}) collective-permute-start(f32[128,16]{0,1:T(8,128)S(1)} %get-tuple-element.14), channel_id=1, source_target_pairs={{1,0},{2,1},{3,2},{5,4},{6,5},{7,6},{9,8},{10,9},{11,10},{13,12},{... | collective-permute-start | bytes 24584 | tf_op jit(solution)/shard_map/ppermute | solution.py:13
  127.2 3.7 %collective-permute-start.2 = (f32[128,16]{0,1:T(8,128)S(1)}, f32[128,16]{0,1:T(8,128)S(1)}, u32[]{:S(2)}, u32[]{:S(2)}) collective-permute-start(f32[128,16]{0,1:T(8,128)S(1)} %get-tuple-element.15), channel_id=1, source_target_pairs={{1,0},{2,1},{3,2},{5,4},{6,5},{7,6},{9,8},{10,9},{11,10},{13,12},{... | collective-permute-start | bytes 24584 | tf_op jit(solution)/shard_map/ppermute | solution.py:13
Sparse Core Ops, SparseCore 0:
  99.8 25.3 reduce-scatter.1
where the time goes:
time: 148 us; the launch traced here: 147 us
  local copies, waits for them, and re-layouts  63.6 us (43%)
  matrix products  27.5 us (19%)
  waiting for transfers between devices  26.3 us (18%)
  between operations  14.1 us (10%)
  blocking collectives  8.56 us (6%)
  starting transfers between devices  3.9 us (3%)
  other arithmetic  3.19 us (2%)
    reshape x2, local copies, waits for them, and re-layouts, hankel(): return repeated.reshape(row_total, delay_span, length + 1)[:, :, :block_len]  25.5 us
    reduce_scatter x1, waiting for transfers between devices, on_device(): lax.psum_scatter(project_lags(slopes, offset_local, local_x, local_s, del...  25.5 us
    pad x2, local copies, waits for them, and re-layouts, hankel(): repeated = jnp.pad(repeated, ((0, 0), (0, delay_span)))  21.1 us
    dot_general x1, matrix products, project_lags(): jnp.einsum('prk,rkt->pt', onehot, lagged_x, preferred_element_type=jnp.fl...  14.7 us
    dot_general x1, matrix products, project_lags(): jnp.einsum('prk,rkt->pt', onehot, lagged_s, preferred_element_type=jnp.fl...  12.9 us
    another operation x2, local copies, waits for them, and re-layouts, hankel(): repeated = jnp.tile(samples, (1, delay_span))  12.1 us
    pmax x1, blocking collectives, on_device(): peak_values = lax.pmax(jnp.max(coherence, axis=1), ('ta', 'af'))  8.56 us
    ppermute x3, starting transfers between devices, passed_along(): lax.ppermute(value, axis, [(source, source + steps) for source in range(l...  3.86 us
  transfers between devices with their start and end apart: 4, of which 2 were waited for; matrix products, arithmetic and copies ran while one was open for 3% of the time, Pallas kernels for 0%

commit v1 on v0

v1 whole, which is shorter than its diff:
```python
import functools

import jax
import jax.numpy as jnp
from jax import lax
from jax.experimental import pallas as pl
from jax.experimental.pallas import tpu as pltpu
from jax.sharding import PartitionSpec as P

SPAN = 64
WIN = 16
GROUP = 4
PACK = 16


def passed_along(value, axis, steps):
    count = lax.axis_size(axis)
    leading, last = (max(0, -steps), min(count, count - steps))
    return lax.ppermute(value, axis, [(source, source + steps) for source in range(leading, last)])


def stack_kernel(traces, halo, gain, offsets, slopes, out, samples, shifted, delays, acc, *, cols, row_blk, col_blk):
    rows, block_len = traces.shape
    rest = halo.shape[1]
    slows = slopes.shape[1]
    weighted = jnp.concatenate(
        [traces[...].astype(jnp.float32), halo[...].astype(jnp.float32)], axis=1
    ) * gain[...].astype(jnp.float32)
    turned = weighted.T
    filled = block_len + rest
    samples[0, 0:filled, :] = turned
    samples[1, 0:filled, :] = (turned * turned).astype(jnp.bfloat16).astype(jnp.float32)
    delays[...] = ((offsets[...] * slopes[...]) >> 16).astype(jnp.float32).astype(jnp.bfloat16)
    reach = shifted.shape[2]
    for phase in range(PACK):
        shifted[phase] = samples[:, phase : phase + reach, :].astype(jnp.bfloat16)
    acc[...] = jnp.zeros_like(acc)
    for row in range(0, rows, row_blk):
        for col in range(0, slows, col_blk):

            def body(step, carry, row=row, col=col):
                first = step * GROUP
                left, right = [], []
                here = delays[row : row + row_blk, col : col + col_blk]
                for lag in range(GROUP):
                    at = first + lag
                    start = pl.multiple_of((at // PACK) * PACK, PACK)
                    part = [
                        shifted[at % PACK, half, pl.ds(start, cols), row : row + row_blk] for half in range(2)
                    ]
                    left.append(jnp.concatenate(part, axis=0))
                    hit = here == at.astype(jnp.float32).astype(jnp.bfloat16)
                    right.append(jnp.where(hit, jnp.bfloat16(1), jnp.bfloat16(0)))
                acc[:, col : col + col_blk] += jnp.dot(
                    jnp.concatenate(left, axis=1),
                    jnp.concatenate(right, axis=0),
                    preferred_element_type=jnp.float32,
                )
                return carry

            lax.fori_loop(0, SPAN // GROUP, body, 0)
    groups, _, width = out.shape
    for group in range(groups):
        out[group] = acc[:, group * width : (group + 1) * width]


def semblance_kernel(parts, stack, coherence, peak, sums, *, cols, block_len):
    total = parts[0]
    for group in range(1, parts.shape[0]):
        total = total + parts[group]
    power = total[:cols] * total[:cols]
    energy = total[cols:]
    stack[...] = total[:block_len].T
    sums[0] = power
    sums[1] = energy
    length, reach = cols, 1
    while reach < WIN:
        length = length - reach
        sums[:, 0:length] = sums[:, 0:length] + sums[:, reach : reach + length]
        reach *= 2
    result = sums[0, 0:block_len] / jnp.maximum(sums[1, 0:block_len], 1.0)
    coherence[...] = result.T
    peak[...] = jnp.max(result, axis=0, keepdims=True)


def largest(value, axes):
    for axis in axes[::-1]:
        count = lax.axis_size(axis)
        step = 1
        if count & (count - 1):
            value = lax.pmax(value, axis)
            continue
        while step < count:
            other = lax.ppermute(value, axis, [(i, i ^ step) for i in range(count)])
            value = jnp.maximum(value, other)
            step *= 2
    return value


def on_device(traces, slopes, offsets, live):
    receiver_group = lax.axis_index("rx")
    groups = lax.axis_size("rx")
    rows, block_len = traces.shape
    slows = slopes.shape[0]
    width = slows // groups
    rest = SPAN + WIN
    cols = block_len + WIN
    halo = passed_along(traces[:, :rest], ("ta", "af"), -1)
    gain = lax.dynamic_slice_in_dim(live, receiver_group * rows, rows)
    offset_local = lax.dynamic_slice_in_dim(offsets, receiver_group * rows, rows)
    row_blk, col_blk = min(256, rows), min(256, slows)
    partial = pl.pallas_call(
        functools.partial(stack_kernel, cols=cols, row_blk=row_blk, col_blk=col_blk),
        out_shape=jax.ShapeDtypeStruct((groups, 2 * cols, width), jnp.float32),
        scratch_shapes=[
            pltpu.VMEM((2, block_len + rest, rows), jnp.float32),
            pltpu.VMEM((PACK, 2, block_len + rest - PACK, rows), jnp.bfloat16),
            pltpu.VMEM((rows, slows), jnp.bfloat16),
            pltpu.VMEM((2 * cols, slows), jnp.float32),
        ],
        name="stack",
    )(traces, halo, gain[:, None], offset_local[:, None], slopes[None, :])
    parts = lax.all_to_all(partial, "rx", split_axis=0, concat_axis=0, tiled=True)
    stack, coherence, peak = pl.pallas_call(
        functools.partial(semblance_kernel, cols=cols, block_len=block_len),
        out_shape=(
            jax.ShapeDtypeStruct((width, block_len), jnp.float32),
            jax.ShapeDtypeStruct((width, block_len), jnp.float32),
            jax.ShapeDtypeStruct((1, width), jnp.float32),
        ),
        scratch_shapes=[pltpu.VMEM((2, cols, width), jnp.float32)],
        name="semblance",
    )(parts)
    return (stack, coherence, largest(peak, ("ta", "af")).reshape(width))


def solution(mesh):
    placed = (P(("shots", "rx"), ("ta", "af")), P(), P("shots"), P("shots"))
    return jax.shard_map(
        on_device,
        mesh=mesh,
        in_specs=placed,
        out_specs=(
            P(("shots", "rx"), ("ta", "af")),
            P(("shots", "rx"), ("ta", "af")),
            P(("shots", "rx")),
        ),
        check_vma=False,
    )
```

time: 148 us -> 62 us (0.42)
  local copies, waits for them, and re-layouts: 63.6 us -> 4.55 us
  matrix products: 27.5 us -> 0 us
  Pallas kernels: 0 us -> 26.7 us
  waiting for transfers between devices: 26.3 us -> 2.5 us
  blocking collectives: 8.56 us -> 23.2 us
  between operations: 14.1 us -> 0.65 us
  other arithmetic: 3.19 us -> 0.52 us
    dot_general x2 -> x0, matrix products: 27.5 us -> none  [the longest x1 14.7 us: project_lags(): jnp.einsum('prk,rkt->pt', onehot, lagged_x, preferred_element_type=jnp.fl...]
    pallas_call x0 -> x2, Pallas kernels: none -> 26.7 us  [the longest x1 24.9 us: on_device(): pl.pallas_call(functools.partial(stack_kernel, cols=cols, row_blk=row_blk...]
    reshape x2 -> x0, local copies, waits for them, and re-layouts: 25.5 us -> none  [hankel(): return repeated.reshape(row_total, delay_span, length + 1)[:, :, :block_len]]
    reduce_scatter x1 -> x0, waiting for transfers between devices: 25.5 us -> none  [on_device(): lax.psum_scatter(project_lags(slopes, offset_local, local_x, local_s, del...]
    all_to_all x0 -> x1, blocking collectives: none -> 23.2 us  [on_device(): lax.all_to_all(partial, 'rx', split_axis=0, concat_axis=0, tiled=True)]
    pad x2 -> x0, local copies, waits for them, and re-layouts: 21.1 us -> none  [hankel(): repeated = jnp.pad(repeated, ((0, 0), (0, delay_span)))]
    another operation x2 -> x0, local copies, waits for them, and re-layouts: 12.1 us -> none  [hankel(): repeated = jnp.tile(samples, (1, delay_span))]
    pmax x1 -> x0, blocking collectives: 8.56 us -> none  [on_device(): peak_values = lax.pmax(jnp.max(coherence, axis=1), ('ta', 'af'))]
  transfers between devices with their start and end apart: 4 -> 3, of which waited for: 2 -> 2; matrix products, arithmetic and copies ran while one was open for 3% -> 5% of each run, Pallas kernels for 0% -> 0%
where the time goes in v1:
time: 62 us; the launch traced here: 61.7 us
  Pallas kernels  26.7 us (43%)
  blocking collectives  23.2 us (37%)
  local copies, waits for them, and re-layouts  4.55 us (7%)
  starting transfers between devices  3.58 us (6%)
  waiting for transfers between devices  2.5 us (4%)
  between operations  0.65 us (1%)
    pallas_call x1, Pallas kernels, on_device(): pl.pallas_call(functools.partial(stack_kernel, cols=cols, row_blk=row_blk...  24.9 us
    all_to_all x1, blocking collectives, on_device(): lax.all_to_all(partial, 'rx', split_axis=0, concat_axis=0, tiled=True)  23.2 us
    ppermute x2, waiting for transfers between devices, largest(): other = lax.ppermute(value, axis, [(i, i ^ step) for i in range(count)])  2.49 us
    ppermute x2, starting transfers between devices, largest(): other = lax.ppermute(value, axis, [(i, i ^ step) for i in range(count)])  2.28 us
    pallas_call x1, Pallas kernels, on_device(): pl.pallas_call(functools.partial(semblance_kernel, cols=cols, block_len=b...  1.86 us
    unnamed x4, local copies, waits for them, and re-layouts  1.31 us
    ppermute x1, starting transfers between devices, passed_along(): lax.ppermute(value, axis, [(source, source + steps) for source in range(l...  1.29 us
  transfers between devices with their start and end apart: 3, of which 2 were waited for; matrix products, arithmetic and copies ran while one was open for 5% of the time, Pallas kernels for 0%

profile of v1, /device:TPU:0, one launch (start us, length us, event | category | flops | bytes accessed | tf_op | source)
XLA Modules:
  0.0 61.7 jit_solution(13006478864790643649)
XLA Ops:
  0.6 1.3 %collective-permute-start = (bf16[512,80]{1,0:T(8,128)(2,1)}, bf16[512,80]{1,0:T(8,128)(2,1)S(1)}, u32[]{:S(2)}, u32[]{:S(2)}) collective-permute-start(bf16[512,80]{1,0:T(8,128)(2,1)} %bitcast.6), channel_id=1, source_target_pairs={{1,0},{2,1},{3,2},{5,4},{6,5},{7,6},{9,8},{10,9},{11,10},{13,12},{... | collective-permute-start | bytes 245768 | tf_op jit(solution)/shard_map/ppermute | solution.py:19
  1.9 0.8 %dynamic_slice.7 = s32[512]{0:T(512)S(1)} dynamic-slice(s32[2048]{0:T(1024)} %param.6, s32[]{:T(128)S(6)} %select_n.4), dynamic_slice_sizes={512} | dynamic-slice | bytes 4100 | tf_op jit(solution)/shard_map/dynamic_slice | solution.py:110
  2.7 0.8 %dynamic_slice.6 = s32[512]{0:T(512)S(1)} dynamic-slice(s32[2048]{0:T(1024)} %param.7, s32[]{:T(128)S(6)} %select_n.4), dynamic_slice_sizes={512} | dynamic-slice | bytes 4100 | tf_op jit(solution)/shard_map/dynamic_slice | solution.py:109
  3.5 0.9 %copy.7.gain = s32[512,1]{1,0:T(8,128)} copy(s32[512,1]{0,1:T(1,128)S(1)} %bitcast.8) | data formatting | bytes 4096 | tf_op jit(solution)/shard_map/broadcast_in_dim | solution.py:122
  4.3 0.8 %copy.8.offsets = s32[512,1]{1,0:T(8,128)} copy(s32[512,1]{0,1:T(1,128)S(1)} %bitcast.7) | data formatting | bytes 4096 | tf_op jit(solution)/shard_map/broadcast_in_dim | solution.py:122
  5.2 0.0 collective-permute-done.halo
  5.2 0.0 copy-start
  5.2 0.7 %copy-done = bf16[512,80]{1,0:T(8,128)(2,1)} copy-done((bf16[512,80]{1,0:T(8,128)(2,1)}, bf16[512,80]{1,0:T(8,128)(2,1)S(1)}, u32[]{:S(2)}) %copy-start) | copy-done | bytes 81944
  5.8 24.9 %stack.1 = f32[4,288,128]{2,1,0:T(8,128)} custom-call(bf16[512,128]{1,0:T(8,128)(2,1)} %traces.1, bf16[512,80]{1,0:T(8,128)(2,1)} %copy-done, s32[512,1]{1,0:T(8,128)} %copy.7.gain, s32[512,1]{1,0:T(8,128)} %copy.8.offsets, s32[1,512]{1,0:T(1,128)} %bitcast.9), custom_call_target="tpu_custom_call" | custom-call | tf_op jit(solution)/shard_map/stack/pallas_call | solution.py:112
  30.7 23.2 %all_to_all.5.parts = f32[4,288,128]{2,1,0:T(8,128)} all-to-all(f32[4,288,128]{2,1,0:T(8,128)} %stack.1), channel_id=1, replica_groups=mesh['shots'=2,'rx'=4,'ta'=2,'af'=2] {'rx'}, dimensions={0} | all-to-all | bytes 1179648 | tf_op jit(solution)/shard_map/all_to_all | solution.py:123
  53.9 1.9 %semblance.1 = (f32[128,128]{1,0:T(8,128)}, f32[128,128]{1,0:T(8,128)}, f32[1,128]{1,0:T(1,128)}) custom-call(f32[4,288,128]{2,1,0:T(8,128)} %all_to_all.5.parts), custom_call_target="tpu_custom_call" | custom-call | tf_op jit(solution)/shard_map/semblance/pallas_call | solution.py:124
  55.7 0.0 copy-start.1
  55.8 0.7 %copy-done.1 = f32[1,128]{1,0:T(1,128)S(1)} copy-done((f32[1,128]{1,0:T(1,128)S(1)}, f32[1,128]{1,0:T(1,128)}, u32[]{:S(2)}) %copy-start.1) | copy-done | bytes 536
  56.4 0.4 collective-permute-start.1
  56.8 0.8 %collective-permute-done.1 = f32[1,128]{1,0:T(1,128)S(1)} collective-permute-done((f32[1,128]{1,0:T(1,128)S(1)}, f32[1,128]{1,0:T(1,128)S(1)}, u32[]{:S(2)}, u32[]{:S(2)}) %collective-permute-start.1) | collective-permute-done | bytes 544 | tf_op jit(solution)/shard_map/ppermute | solution.py:94
  57.6 1.9 %collective-permute-start.2 = (f32[1,128]{1,0:T(1,128)S(1)}, f32[1,128]{1,0:T(1,128)S(1)}, u32[]{:S(2)}, u32[]{:S(2)}) collective-permute-start(f32[1,128]{1,0:T(1,128)S(1)} %max.6), channel_id=1, source_target_pairs={{0,2},{2,0},{1,3},{3,1},{4,6},{6,4},{5,7},{7,5},{8,10},{10,8},{9,1... | collective-permute-start | bytes 1544 | tf_op jit(solution)/shard_map/ppermute | solution.py:94
  59.5 1.7 %collective-permute-done.2 = f32[1,128]{1,0:T(1,128)S(1)} collective-permute-done((f32[1,128]{1,0:T(1,128)S(1)}, f32[1,128]{1,0:T(1,128)S(1)}, u32[]{:S(2)}, u32[]{:S(2)}) %collective-permute-start.2) | collective-permute-done | bytes 544 | tf_op jit(solution)/shard_map/ppermute | solution.py:94
  61.2 0.5 maximum_bitcast_fusion
  (1 shorter events, 0.0 us)
Async XLA Ops:
  0.6 4.5 %collective-permute-start = (bf16[512,80]{1,0:T(8,128)(2,1)}, bf16[512,80]{1,0:T(8,128)(2,1)S(1)}, u32[]{:S(2)}, u32[]{:S(2)}) collective-permute-start(bf16[512,80]{1,0:T(8,128)(2,1)} %bitcast.6), channel_id=1, source_target_pairs={{1,0},{2,1},{3,2},{5,4},{6,5},{7,6},{9,8},{10,9},{11,10},{13,12},{... | collective-permute-start | bytes 245768 | tf_op jit(solution)/shard_map/ppermute | solution.py:19
  5.2 0.7 %copy-start = (bf16[512,80]{1,0:T(8,128)(2,1)}, bf16[512,80]{1,0:T(8,128)(2,1)S(1)}, u32[]{:S(2)}) copy-start(bf16[512,80]{1,0:T(8,128)(2,1)S(1)} %collective-permute-done.halo) | copy-start | bytes 245764
  55.7 0.7 %copy-start.1 = (f32[1,128]{1,0:T(1,128)S(1)}, f32[1,128]{1,0:T(1,128)}, u32[]{:S(2)}) copy-start(f32[1,128]{1,0:T(1,128)} %get-tuple-element.8) | copy-start | bytes 1540
  56.4 1.2 %collective-permute-start.1 = (f32[1,128]{1,0:T(1,128)S(1)}, f32[1,128]{1,0:T(1,128)S(1)}, u32[]{:S(2)}, u32[]{:S(2)}) collective-permute-start(f32[1,128]{1,0:T(1,128)S(1)} %copy-done.1), channel_id=1, source_target_pairs={{0,1},{1,0},{2,3},{3,2},{4,5},{5,4},{6,7},{7,6},{8,9},{9,8},{10,11... | collective-permute-start | bytes 1544 | tf_op jit(solution)/shard_map/ppermute | solution.py:94
  57.6 3.6 %collective-permute-start.2 = (f32[1,128]{1,0:T(1,128)S(1)}, f32[1,128]{1,0:T(1,128)S(1)}, u32[]{:S(2)}, u32[]{:S(2)}) collective-permute-start(f32[1,128]{1,0:T(1,128)S(1)} %max.6), channel_id=1, source_target_pairs={{0,2},{2,0},{1,3},{3,1},{4,6},{6,4},{5,7},{7,5},{8,10},{10,8},{9,1... | collective-permute-start | bytes 1544 | tf_op jit(solution)/shard_map/ppermute | solution.py:94
